TPU v7x, 32 devices: a whole 2x2x4 slice. The times are simulated.
32 devices in a mesh: chan: 4 (over y, x), rows: 8 (over z, core).
Axes of the slice: x: 2, y: 2, z: 4, core: 2. Of those that a mesh axis runs over, the one named last changes fastest.
Arguments:
- residual: float32 [4, 256, 16384], P('chan', 'rows'), may hold values from -6 to 6
- psf: float32 [4, 2048, 2048], P('chan', 'rows'), may hold values from -2 to 2
- positions: int32 [32, 2], replicated, may hold values from 0 to 15360, as said below
Outputs:
- residual_out: float32 [4, 256, 16384], P('chan', 'rows')
- normalized: float32 [256, 16384], P('rows', 'chan')
Inputs may be any that keep to these rules, and one draw needn't show every extreme that they name: positions[k, 0] is a row of the image, 0 to 255; positions[k, 1] is a column from 1024 to 15360.
All inputs are finite; a program needn't handle non-finite values.
Results may differ from a plain program's by a relative error of at most 0.0001.
Values sent between devices are 32-bit elements; how exact they have to be, the bound alone decides.
A program may use at most 128 MiB of HBM per device.

v0:
```python
import jax
import jax.numpy as jnp
from jax import lax
from jax.sharding import PartitionSpec as P

STEPS = 32


def on_device(residual, psf, positions):
    chan_id = lax.axis_index("chan")
    nchan = lax.axis_size("chan")
    row_id = lax.axis_index("rows")
    nrows = lax.axis_size("rows")
    slab = residual.shape[1]
    ncols = residual.shape[2]
    own_psf = psf[0]
    shard_rows = own_psf.shape[0]
    patch = own_psf.shape[1]
    half = patch // 2
    first = row_id * slab
    chan_hot = (jnp.arange(nchan) == chan_id).astype(jnp.float32)
    full_psf = lax.all_gather(own_psf, "rows", axis=0, tiled=True)
    padded_psf = jnp.pad(full_psf, ((slab, slab), (0, 0)))
    zero = jnp.int32(0)

    def subtract(image, row, col, amount):
        offset = first - row + half
        touches = jnp.logical_and(offset > -slab, offset < patch)
        start = jnp.clip(offset + slab, 0, patch + slab)
        psf_rows = lax.dynamic_slice(padded_psf, (start, zero), (slab, patch))
        window = lax.dynamic_slice(image, (zero, col - half), (slab, patch))
        scale = jnp.where(touches, amount, 0.0)
        return lax.dynamic_update_slice(image, window - scale * psf_rows, (zero, col - half))

    image = residual[0]
    peak_rows = positions[:, 0]
    peak_cols = positions[:, 1]
    inside = jnp.logical_and(peak_rows >= first, peak_rows < first + slab)
    local_rows = jnp.clip(peak_rows - first, 0, slab - 1)
    start_values = jnp.where(inside, image[local_rows, peak_cols], 0.0)
    row_offset = peak_rows[:, None] - peak_rows[None, :] + half - row_id * shard_rows
    col_offset = peak_cols[:, None] - peak_cols[None, :] + half
    owned = (row_offset >= 0) & (row_offset < shard_rows) & (col_offset >= 0) & (col_offset < patch)
    couple = own_psf[jnp.clip(row_offset, 0, shard_rows - 1), jnp.clip(col_offset, 0, patch - 1)]
    couple = jnp.where(owned, couple, 0.0)
    start_table, couple_table = lax.psum(
        (chan_hot[:, None] * start_values[None, :], chan_hot[:, None, None] * couple[None, :, :]),
        ("chan", "rows"),
    )

    def solve(k, amps):
        taken = jnp.sum(amps * lax.dynamic_index_in_dim(couple_table, k, 1, False), axis=1)
        value = lax.dynamic_index_in_dim(start_table, k, 1, False) - taken
        amp = 0.25 * (value + jnp.sum(value) / nchan)
        return lax.dynamic_update_index_in_dim(amps, amp, k, 1)

    amps = lax.fori_loop(0, STEPS, solve, jnp.zeros((nchan, STEPS), jnp.float32))
    own_amps = jnp.sum(chan_hot[:, None] * amps, axis=0)

    def apply(k, image):
        return subtract(image, positions[k, 0], positions[k, 1], own_amps[k])

    image = lax.fori_loop(0, STEPS, apply, image)
    count = slab * nrows * ncols
    parts = lax.psum_scatter(image, "chan", scatter_dimension=1, tiled=True)
    total = lax.psum(jnp.sum(parts * parts), ("chan", "rows"))
    normalized = parts * lax.rsqrt(total / count + 1e-06)
    return (image[None], normalized)


def solution(mesh):
    return jax.shard_map(
        on_device,
        mesh=mesh,
        in_specs=(P("chan", "rows", None), P("chan", "rows", None), P()),
        out_specs=(P("chan", "rows", None), P("rows", "chan")),
        check_vma=False,
    )
```

profile of v0, /device:TPU:0, one launch (start us, length us, event | category | flops | bytes accessed | tf_op | source)
XLA Modules:
  0.0 488.5 jit_solution(8474311670628880495)
XLA Ops:
  7.2 3.0 copy.28
  11.9 8.6 %gather_fusion.1 = f32[1024]{0:T(1024)S(1)} fusion(f32[256,2048]{1,0:T(8,128)S(1)} %bitcast.46, s32[1024]{0:T(1024)S(1)} %reshape.252), kind=kCustom, calls=%fused_computation.1 | custom fusion | bytes 16384 | tf_op jit(solution)/shard_map/gather | solution.py:44
  20.5 1.7 gather_fusion
  22.5 50.0 %all-reduce.1 = (f32[4,32]{1,0:T(4,128)S(1)}, f32[4,32,32]{2,0,1:T(4,128)S(1)}) all-reduce(f32[4,32]{1,0:T(4,128)S(1)} %broadcast_multiply_fusion.2, f32[4,32,32]{2,0,1:T(4,128)S(1)} %broadcast_multiply_fusion.1), channel_id=1, replica_groups=mesh['chan'=4,'rows'=8] {'chan','rows'}, use_global_device_ids=true, to_apply=%region_1.2 | all-reduce | flops 4224 | bytes 33792 | tf_op jit(solution)/shard_map/psum | solution.py:46
  72.5 57.8 %while.30 = (s32[]{:T(128)}, f32[4,32]{1,0:T(4,128)S(1)}, f32[4,32]{1,0:T(4,128)S(1)}, f32[4,32,32]{2,0,1:T(4,128)S(1)}, s32[]{:T(128)}, /*index=5*/f32[]{:T(128)}, s32[]{:T(128)}) while((s32[]{:T(128)}, f32[4,32]{1,0:T(4,128)S(1)}, f32[4,32]{1,0:T(4,128)S(1)}, f32[4,32,32]{2,0,1:T(4,128)S(1)}, s32[]{:T(128)}, /*index=5*/f32[]{:T(128)}, ...), condition=%wide.region_5.6_spmd, body=%wide.region_2.5_spmd.sunk | while | flops 274 | bytes 2329 | solution.py:57
  130.4 34.9 %all-gather.3.cloned.1.call-done = f32[1,2048,2048]{2,1,0:T(8,128)} async-done(((f32[1,256,2048]{2,1,0:T(8,128)}), f32[1,2048,2048]{2,1,0:T(8,128)}) %all-gather.3.cloned.1.call-update) | async-done | bytes 16777232 | tf_op jit(solution)/shard_map/all_gather | solution.py:22
  165.3 11.7 %pad.4 = f32[2112,2048]{1,0:T(8,128)} pad(f32[2048,2048]{1,0:T(8,128)} %bitcast.50, f32[]{:T(128)} %constant.206.clone.1), padding=32_32x0_0 | pad | bytes 34078724 | tf_op jit(solution)/shard_map/jit(_pad)/pad | solution.py:23
  177.0 227.3 %while.31 = (s32[]{:T(128)}, f32[32,16384]{1,0:T(8,128)}, s32[32,2]{0,1:T(2,128)S(1)}, s32[]{:T(128)}, f32[32]{0:T(128)S(1)}, /*index=5*/f32[2112,2048]{1,0:T(8,...) while((s32[]{:T(128)}, f32[32,16384]{1,0:T(8,128)}, ...), condition=%wide.region_8.9_spmd, body=%wide.region_7.8_spmd.sunk | while | flops 131087 | bytes 1311065 | solution.py:63
  180.9 1.2 multiply_subtract_fusion.2
  182.1 2.0 dynamic_update_slice.24
  188.0 1.2 multiply_subtract_fusion.2
  189.2 2.0 dynamic_update_slice.24
  195.2 1.2 multiply_subtract_fusion.2
  196.4 2.0 dynamic_update_slice.24
  202.3 1.2 multiply_subtract_fusion.2
  203.5 1.9 dynamic_update_slice.24
  209.3 1.2 multiply_subtract_fusion.2
  210.5 2.0 dynamic_update_slice.24
  216.5 1.2 multiply_subtract_fusion.2
  217.7 2.0 dynamic_update_slice.24
  223.6 1.2 multiply_subtract_fusion.2
  224.8 2.0 dynamic_update_slice.24
  230.7 1.2 multiply_subtract_fusion.2
  231.9 2.0 dynamic_update_slice.24
  237.9 1.2 multiply_subtract_fusion.2
  239.1 2.0 dynamic_update_slice.24
  244.9 1.2 multiply_subtract_fusion.2
  246.1 2.0 dynamic_update_slice.24
  252.0 1.2 multiply_subtract_fusion.2
  253.2 2.0 dynamic_update_slice.24
  259.2 1.2 multiply_subtract_fusion.2
  260.4 2.0 dynamic_update_slice.24
  266.3 1.2 multiply_subtract_fusion.2
  267.5 2.0 dynamic_update_slice.24
  273.4 1.2 multiply_subtract_fusion.2
  274.6 2.0 dynamic_update_slice.24
  280.5 1.2 multiply_subtract_fusion.2
  281.7 2.0 dynamic_update_slice.24
  287.6 1.2 multiply_subtract_fusion.2
  288.8 2.0 dynamic_update_slice.24
  294.8 1.2 multiply_subtract_fusion.2
  296.0 2.0 dynamic_update_slice.24
  301.9 1.2 multiply_subtract_fusion.2
  303.1 2.0 dynamic_update_slice.24
  310.2 1.7 dynamic_update_slice.24
  315.8 1.2 multiply_subtract_fusion.2
  317.0 2.0 dynamic_update_slice.24
  323.0 1.2 multiply_subtract_fusion.2
  324.2 2.0 dynamic_update_slice.24
  331.3 2.0 dynamic_update_slice.24
  338.3 2.0 dynamic_update_slice.24
  345.5 2.0 dynamic_update_slice.24
  352.6 2.0 dynamic_update_slice.24
  359.7 2.0 dynamic_update_slice.24
  366.9 2.0 dynamic_update_slice.24
  374.0 2.0 dynamic_update_slice.24
  381.1 2.0 dynamic_update_slice.24
  388.3 1.8 dynamic_update_slice.24
  395.1 2.0 dynamic_update_slice.24
  402.3 2.0 dynamic_update_slice.24
  404.3 33.5 %reduce-scatter.2.cloned.1.call-done = f32[32,4096]{1,0:T(8,128)} async-done(((f32[32,16384]{1,0:T(8,128)}), f32[32,4096]{1,0:T(8,128)}) %reduce-scatter.2.cloned.1.call-update) | async-done | bytes 524304 | tf_op jit(solution)/shard_map/reduce_scatter | solution.py:65
  437.9 1.8 multiply_reduce_fusion
  439.6 39.5 %psum.23 = f32[]{:T(128)} all-reduce(f32[]{:T(128)} %multiply_reduce_fusion), channel_id=1, replica_groups=mesh['chan'=4,'rows'=8] {'chan','rows'}, use_global_device_ids=true, to_apply=%region_11.12 | all-reduce | flops 1 | bytes 8 | tf_op jit(solution)/shard_map/psum | solution.py:66
  479.8 1.9 broadcast_multiply_fusion
  (287 shorter events, 91.3 us)
Async XLA Ops:
  7.2 158.1 %all-gather.3.cloned.1.call-start = ((), (), s32[]{:S(2)}) async-start(), calls=%async_computation.2 | async-start | bytes 18874368 | tf_op jit(solution)/shard_map/all_gather | solution.py:22
  10.3 0.7 copy-start.1
  10.3 1.6 copy-start
  10.3 427.6 %reduce-scatter.2.cloned.1.call-start = ((), (), s32[]{:S(2)}) async-start(), calls=%async_computation.1 | async-start | bytes 2621440 | tf_op jit(solution)/shard_map/reduce_scatter | solution.py:65
Sparse Core Ops, SparseCore 0:
  10.4 154.8 all-gather.2
  404.5 33.3 reduce-scatter.1
where the time goes:
time: 492 us; the launch traced here: 489 us
  local copies, waits for them, and re-layouts  139 us (28%)
  loops' own time  108 us (22%)
  blocking collectives  89.5 us (18%)
  other arithmetic  68.9 us (14%)
  waiting for transfers between devices  68.4 us (14%)
  between operations  14.8 us (3%)
    another operation x1, loops' own time, on_device(): image = lax.fori_loop(0, STEPS, apply, image)  85.1 us
    dynamic_update_slice x32, local copies, waits for them, and re-layouts, subtract(): lax.dynamic_update_slice(image, window - scale * psf_rows, (zero, col - h...  64.1 us
    psum x1, blocking collectives, on_device(): lax.psum((chan_hot[:, None] * start_values[None, :], chan_hot[:, None, No...  50 us
    dynamic_slice x64, local copies, waits for them, and re-layouts, apply(): return subtract(image, positions[k, 0], positions[k, 1], own_amps[k])  39.7 us
    psum x1, blocking collectives, on_device(): total = lax.psum(jnp.sum(parts * parts), ('chan', 'rows'))  39.5 us
    sub x32, other arithmetic, subtract(): window - scale * psf_rows  38.4 us
    all_gather x1, waiting for transfers between devices, on_device(): full_psf = lax.all_gather(own_psf, 'rows', axis=0, tiled=True)  34.9 us
    reduce_scatter x1, waiting for transfers between devices, on_device(): parts = lax.psum_scatter(image, 'chan', scatter_dimension=1, tiled=True)  33.5 us
  transfers between devices with their start and end apart: 2, of which 2 were waited for; matrix products, arithmetic and copies ran while one was open for 9% of the time, Pallas kernels for 0%

commit v1 on v0

--- a/solution.py
+++ b/solution.py
@@ -1,12 +1,492 @@
+import functools
+
 import jax
 import jax.numpy as jnp
 from jax import lax
+from jax.experimental import pallas as pl
+from jax.experimental.pallas import tpu as pltpu
 from jax.sharding import PartitionSpec as P
 
 STEPS = 32
+LANES = 128
+PIECES = 4
+MESH = pl.DeviceIdType.MESH
+
+
+def at(start, size):
+    return pl.ds(pl.multiple_of(start, 8), size)
+
+
+def pick(ref, row, col, wanted, lane_to, acc):
+    place = (pl.ds(pl.multiple_of((row >> 3) << 3, 8), 8), pl.ds(pl.multiple_of((col >> 7) << 7, LANES), LANES))
+    tile = pltpu.roll(ref[place], (lane_to - col) & (LANES - 1), 1)
+    number = lax.broadcasted_iota(jnp.int32, (8, LANES), 0) * LANES + lax.broadcasted_iota(jnp.int32, (8, LANES), 1)
+    return jnp.where(number == jnp.where(wanted, (row & 7) * LANES + lane_to, -1), tile, acc)
+
+
+def table_kernel(pos, res, psf, start, couple, res_v, psf_v, sems):
+    row, nrows = lax.axis_index("rows"), lax.axis_size("rows")
+    slab, steps = res.shape[1], pos.shape[0]
+    shard, patch = psf.shape[1:]
+    half = patch // 2
+    first = row * slab
+    is_root = jnp.logical_or(row == nrows // 2 - 1, row == nrows // 2)
+    loads = [pltpu.make_async_copy(res.at[0], res_v, sems.at[0]), pltpu.make_async_copy(psf.at[0], psf_v, sems.at[1])]
+    loads[0].start()
+
+    @pl.when(is_root)
+    def _():
+        loads[1].start()
+
+    loads[0].wait()
+    acc = jnp.zeros((8, LANES), jnp.float32)
+    for k in range(steps):
+        r = pos[k, 0] - first
+        inside = jnp.logical_and(r >= 0, r < slab)
+        acc = pick(res_v, jnp.clip(r, 0, slab - 1), pos[k, 1], inside, k, acc)
+    start[...] = acc
+
+    @pl.when(is_root)
+    def _():
+        loads[1].wait()
+
+        def fill(k, carry):
+            line = jnp.zeros((8, LANES), jnp.float32)
+            rk = pos[k, 0] + half - row * shard
+            qk = pos[k, 1] + half
+            for j in range(steps):
+                r = rk - pos[j, 0]
+                c = qk - pos[j, 1]
+                owned = (r >= 0) & (r < shard) & (c >= 0) & (c < patch)
+                line = pick(psf_v, jnp.clip(r, 0, shard - 1), jnp.clip(c, 0, patch - 1), owned, j, line)
+            couple[pl.ds(k, 1), :] = jnp.sum(line, axis=0, keepdims=True)
+            return carry
+
+        lax.fori_loop(0, steps, fill, 0)
+
+    @pl.when(jnp.logical_not(is_root))
+    def _():
+        couple[...] = jnp.zeros_like(couple)
+
+
+def make_tables(positions, residual, psf):
+    f32 = jnp.float32
+    anywhere, vmem = pl.BlockSpec(memory_space=pl.ANY), pl.BlockSpec(memory_space=pltpu.VMEM)
+    return pl.pallas_call(
+        table_kernel,
+        out_shape=(jax.ShapeDtypeStruct((8, LANES), f32), jax.ShapeDtypeStruct((positions.shape[0], LANES), f32)),
+        in_specs=[pl.BlockSpec(memory_space=pltpu.SMEM), anywhere, anywhere],
+        out_specs=(vmem, vmem),
+        scratch_shapes=[pltpu.VMEM(residual.shape[1:], f32), pltpu.VMEM(psf.shape[1:], f32), pltpu.SemaphoreType.DMA((2,))],
+        name="make_tables",
+    )(positions, residual, psf)
+
+
+def gather_kernel(nchan, nrows, psf, start_own, couple_own, win, amps_out, psf_v, couple_in, start_in, tables, amps_v,
+                  load_sem, keep_sem, send_sem, recv_sem, pass_sem, start_send, start_recv, couple_sem, table_send, table_recv, amp_send, amp_recv):
+    chan, row = lax.axis_index("chan"), lax.axis_index("rows")
+    chip, core = row // 2, row % 2
+    partner = row + 1 - 2 * core
+    nchips = nrows // 2
+    slab = psf.shape[1] // nrows
+    unit = 2 * slab
+    low, high = nchips - 1, nchips
+    steps = couple_own.shape[0]
+    lane = lax.broadcasted_iota(jnp.int32, (1, LANES), 1)
+
+    load = pltpu.make_async_copy(psf.at[0], psf_v, load_sem)
+    is_low, is_high = row == low, row == high
+    is_root = jnp.logical_or(is_low, is_high)
+
+    @pl.when(is_root)
+    def _():
+        load.start()
+
+    barrier = pltpu.get_barrier_semaphore()
+    for step in range(1, nrows):
+        pl.semaphore_signal(barrier, inc=1, device_id=(chan, (row + step) % nrows), device_id_type=MESH)
+    for step in range(1, nchan):
+        pl.semaphore_signal(barrier, inc=1, device_id=((chan + step) % nchan, row), device_id_type=MESH)
+    pl.semaphore_wait(barrier, nrows + nchan - 2)
+
+    def piece(to_row, z, m, h, index):
+        return pltpu.make_async_remote_copy(
+            src_ref=psf.at[0, pl.ds(index, slab)], dst_ref=win.at[pl.ds(m * unit + h * slab, slab)],
+            send_sem=send_sem.at[z, m, h], recv_sem=recv_sem.at[m, h], device_id=(chan, to_row), device_id_type=MESH)
+
+    def pieces(root, zs):
+        out = []
+        for m in range(nchips + 1):
+            for z in zs:
+                if (z + m < nchips) != (root == low):
+                    continue
+                for h in range(2):
+                    to_row = root ^ 1 if z == root // 2 else 2 * z + h
+                    out.append(piece(to_row, z, m, h, ((z + m) % nchips) * unit + h * slab))
+        return out
+
+    away = {low: [z for z in range(nchips) if z < low // 2], high: [z for z in range(nchips) if z > high // 2]}
+    back = {low: [z for z in range(nchips) if z >= low // 2], high: [z for z in range(nchips) if z <= high // 2]}
+
+    def kept(root):
+        z = root // 2
+        out = []
+        for m in range(nchips + 1):
+            if (z + m < nchips) == (root == low):
+                out.append(pltpu.make_async_copy(psf_v.at[pl.ds(((z + m) % nchips) * unit, unit)], win.at[pl.ds(m * unit, unit)], keep_sem.at[m]))
+        return out
+
+    for root in (low, high):
+        @pl.when(row == root)
+        def _(root=root):
+            for copy in pieces(root, away[root]):
+                copy.start()
+
+    def start_copy(source):
+        return pltpu.make_async_remote_copy(
+            src_ref=start_own, dst_ref=start_in.at[source], send_sem=start_send, recv_sem=start_recv.at[source],
+            device_id=(chan, low), device_id_type=MESH)
+
+    @pl.when(jnp.logical_not(is_low))
+    def _():
+        start_copy(row).start()
+
+    couple_copy = pltpu.make_async_remote_copy(
+        src_ref=couple_own, dst_ref=couple_in, send_sem=couple_sem.at[0], recv_sem=couple_sem.at[1],
+        device_id=(chan, low), device_id_type=MESH)
+
+    @pl.when(is_high)
+    def _():
+        couple_copy.start()
+
+    for root in (low, high):
+        @pl.when(row == root)
+        def _(root=root):
+            for copy in pieces(root, back[root]):
+                copy.start()
+            load.wait()
+            for copy in kept(root):
+                copy.start()
+
+    def amp_copy(step):
+        return pltpu.make_async_remote_copy(
+            src_ref=amps_v, dst_ref=amps_v, send_sem=amp_send.at[step], recv_sem=amp_recv,
+            device_id=(chan, (low + step) % nrows), device_id_type=MESH)
+
+    def table_copy(peer, owner):
+        return pltpu.make_async_remote_copy(
+            src_ref=tables.at[owner], dst_ref=tables.at[owner], send_sem=table_send.at[peer], recv_sem=table_recv.at[owner],
+            device_id=(peer, low), device_id_type=MESH)
+
+    def relay(m):
+        block = at(m * unit + core * slab, slab)
+        return pltpu.make_async_remote_copy(
+            src_ref=win.at[block], dst_ref=win.at[block], send_sem=pass_sem.at[m], recv_sem=recv_sem.at[m, core],
+            device_id=(chan, partner), device_id_type=MESH)
+
+    def arrival(m, h):
+        return pltpu.make_async_remote_copy(
+            src_ref=win.at[at(m * unit + h * slab, slab)], dst_ref=win.at[at(m * unit + h * slab, slab)],
+            send_sem=pass_sem.at[m], recv_sem=recv_sem.at[m, h], device_id=(chan, partner), device_id_type=MESH)
+
+    @pl.when(is_low)
+    def _():
+        total = start_own[...]
+        for step in range(1, nrows):
+            source = (low + step) % nrows
+            start_copy(source).wait_recv()
+            total = total + start_in[source]
+        couple_copy.wait_recv()
+        tables[chan, pl.ds(0, steps), :] = couple_own[...] + couple_in[...]
+        tables[chan, pl.ds(steps, 8), :] = jnp.broadcast_to(jnp.sum(total, axis=0, keepdims=True), total.shape)
+        for step in range(1, nchan):
+            table_copy((chan + step) % nchan, chan).start()
+        for step in range(1, nchan):
+            table_copy((chan + step) % nchan, (chan + step) % nchan).wait_recv()
+        start = jnp.concatenate([tables[c, pl.ds(steps, 1), :] for c in range(nchan)], axis=0)
+
+        def solve(k, amps):
+            couple = jnp.concatenate([tables[c, pl.ds(k, 1), :] for c in range(nchan)], axis=0)
+            value = jnp.sum(jnp.where(lane == k, start, 0.0) - amps * couple, axis=1, keepdims=True)
+            amp = 0.25 * (value + jnp.sum(value, axis=0, keepdims=True) / nchan)
+            return jnp.where(lane == k, amp, amps)
+
+        amps = lax.fori_loop(0, steps, solve, jnp.zeros((nchan, LANES), jnp.float32))
+        amps_v[pl.ds(0, nchan), :] = amps
+        amps_v[pl.ds(nchan, 8 - nchan), :] = jnp.zeros((8 - nchan, LANES), jnp.float32)
+        for step in range(1, nrows):
+            amp_copy(step).start()
+
+    for m in range(nchips + 1):
+        root = jnp.where(chip + m < nchips, low, high)
+        relays = jnp.logical_and(row != root, partner != root)
+
+        @pl.when(relays)
+        def _(m=m):
+            arrival(m, core).wait_recv()
+            relay(m).start()
+
+    for m in range(nchips + 1):
+        root = jnp.where(chip + m < nchips, low, high)
+
+        @pl.when(jnp.logical_and(row != root, partner != root))
+        def _(m=m):
+            arrival(m, 1 - core).wait_recv()
+            relay(m).wait_send()
+
+        @pl.when(partner == root)
+        def _(m=m):
+            arrival(m, 0).wait_recv()
+            arrival(m, 1).wait_recv()
+
+    for root in (low, high):
+        @pl.when(row == root)
+        def _(root=root):
+            for copy in kept(root):
+                copy.wait()
+            for copy in pieces(root, away[root]) + pieces(root, back[root]):
+                copy.wait_send()
+
+    @pl.when(is_high)
+    def _():
+        couple_copy.wait_send()
+
+    @pl.when(is_low)
+    def _():
+        for step in range(1, nchan):
+            table_copy((chan + step) % nchan, chan).wait_send()
+        for step in range(1, nrows):
+            amp_copy(step).wait_send()
+
+    @pl.when(jnp.logical_not(is_low))
+    def _():
+        start_copy(row).wait_send()
+        amp_copy(1).wait_recv()
+
+    amps_out[...] = amps_v[...]
+
+
+def gather_patch(nchan, nrows, psf, start, couple):
+    shard, patch = psf.shape[1:]
+    steps, slab = couple.shape[0], shard // nrows
+    nchips = nrows // 2
+    rows = slab * (nrows + 2)
+    dma, f32 = pltpu.SemaphoreType.DMA, jnp.float32
+    anywhere = pl.BlockSpec(memory_space=pl.ANY)
+    return pl.pallas_call(
+        functools.partial(gather_kernel, nchan, nrows),
+        out_shape=(jax.ShapeDtypeStruct((rows, patch), f32), jax.ShapeDtypeStruct((8, LANES), f32)),
+        in_specs=[anywhere, pl.BlockSpec(memory_space=pltpu.VMEM), pl.BlockSpec(memory_space=pltpu.VMEM)],
+        out_specs=(anywhere, pl.BlockSpec(memory_space=pltpu.VMEM)),
+        scratch_shapes=[
+            pltpu.VMEM((shard, patch), f32), pltpu.VMEM((steps, LANES), f32), pltpu.VMEM((nrows, 8, LANES), f32),
+            pltpu.VMEM((nchan, steps + 8, LANES), f32), pltpu.VMEM((8, LANES), f32),
+            dma, dma((nchips + 1,)), dma((nchips, nchips + 1, 2)), dma((nchips + 1, 2)), dma((nchips + 1,)),
+            dma, dma((nrows,)), dma((2,)), dma((nchan,)), dma((nchan,)), dma((nrows,)), dma,
+        ],
+        compiler_params=pltpu.CompilerParams(collective_id=0, has_side_effects=True),
+        name="gather_patch",
+    )(psf, start, couple)
+
+
+def apply_kernel(pos, amps, res, win, out, image, patch_v, sems):
+    chan, row = lax.axis_index("chan"), lax.axis_index("rows")
+    nrows = lax.axis_size("rows")
+    slab, ncols = res.shape[1], res.shape[2]
+    rows, patch = win.shape
+    chunks = patch // LANES
+    loads = [pltpu.make_async_copy(win.at[:, pl.ds(c * LANES, LANES)], patch_v.at[c], sems.at[c]) for c in range(chunks)]
+    loads.append(pltpu.make_async_copy(res.at[0], image.at[:, pl.ds(0, ncols)], sems.at[chunks]))
+    for copy in loads:
+        copy.start()
+    for copy in loads:
+        copy.wait()
+    lane = lax.broadcasted_iota(jnp.int32, (8, LANES), 1)
+    top = (row % 2) * slab + slab * nrows
+
+    def step(k, carry):
+        amp = amps[chan, k]
+        begin = top - pos[k, 0]
+        left = pos[k, 1] - patch // 2
+        shift = left & (LANES - 1)
+        base = left - shift
+        keep = lane < shift
+        for t in range(slab // 8):
+            before = jnp.zeros((8, LANES), jnp.float32)
+            for c in range(chunks + 1):
+                now = jnp.zeros((8, LANES), jnp.float32)
+                if c < chunks:
+                    now = pltpu.roll(patch_v[c, pl.ds(begin + 8 * t, 8), :] * amp, shift, 1)
+                place = (pl.ds(8 * t, 8), pl.ds(pl.multiple_of(base + c * LANES, LANES), LANES))
+                image[place] = image[place] - jnp.where(keep, before, now)
+                before = now
+        return carry
+
+    lax.fori_loop(0, pos.shape[0], step, 0)
+    store = pltpu.make_async_copy(image.at[:, pl.ds(0, ncols)], out.at[0], sems.at[0])
+    store.start()
+    store.wait()
+
+
+def apply_peaks(positions, amps, residual, win):
+    slab, ncols = residual.shape[1:]
+    rows, patch = win.shape
+    chunks = patch // LANES
+    anywhere, scalars = pl.BlockSpec(memory_space=pl.ANY), pl.BlockSpec(memory_space=pltpu.SMEM)
+    return pl.pallas_call(
+        apply_kernel,
+        out_shape=jax.ShapeDtypeStruct(residual.shape, jnp.float32),
+        in_specs=[scalars, scalars, anywhere, anywhere],
+        out_specs=anywhere,
+        scratch_shapes=[
+            pltpu.VMEM((slab, ncols + LANES), jnp.float32), pltpu.VMEM((chunks, rows, LANES), jnp.float32),
+            pltpu.SemaphoreType.DMA((chunks + 1,)),
+        ],
+        name="apply_peaks",
+    )(positions, amps, residual, win)
+
+
+def sum_kernel(nchan, nrows, count, image, out, own, near, first_far, first_own, passed, second, squares,
+               load_sem, far_send, far_recv, own_send, own_recv, pass_send, pass_recv, square_send, square_recv):
+    chan, row = lax.axis_index("chan"), lax.axis_index("rows")
+    me = row * nchan + chan
+    slab, ncols = image.shape[1], image.shape[2]
+    cols = ncols // nchan
+    part = slab // 2
+    width = cols // PIECES
+    bits = ((1, 2), (2, 1))
+
+    def block(c):
+        return pl.ds(pl.multiple_of(c * cols, LANES), cols)
+
+    def flip(bit):
+        if bit == 1:
+            return chan + 1 - 2 * (chan % 2)
+        return (chan + 2) % 4
+
+    diagonal = 3 - chan
+    loads = [pltpu.make_async_copy(image.at[0, :, block(chan)], own, load_sem.at[0])]
+    for p in range(2):
+        loads.append(pltpu.make_async_copy(image.at[0, pl.ds(p * part, part), block(flip(bits[p][1]))], near.at[p], load_sem.at[1 + p]))
+    for copy in loads:
+        copy.start()
+
+    barrier = pltpu.get_barrier_semaphore()
+    for step in range(1, nrows * nchan):
+        other = (me + step) % (nrows * nchan)
+        pl.semaphore_signal(barrier, inc=1, device_id=(other % nchan, other // nchan), device_id_type=MESH)
+    pl.semaphore_wait(barrier, nrows * nchan - 1)
+
+    def send(p, g, source, dest, send_sem, recv_sem, to):
+        return pltpu.make_async_remote_copy(
+            src_ref=source, dst_ref=dest.at[p, :, pl.ds(g * width, width)], send_sem=send_sem.at[p, g], recv_sem=recv_sem.at[p, g],
+            device_id=(to, row), device_id_type=MESH)
+
+    def tile(p, g, c):
+        return image.at[0, pl.ds(p * part, part), pl.ds(pl.multiple_of(c * cols + g * width, LANES), width)]
+
+    def far(p, g):
+        return send(p, g, tile(p, g, diagonal), first_far, far_send, far_recv, flip(bits[p][0]))
+
+    def mine(p, g):
+        return send(p, g, tile(p, g, flip(bits[p][0])), first_own, own_send, own_recv, flip(bits[p][0]))
+
+    def onward(p, g):
+        return send(p, g, passed.at[p, :, pl.ds(g * width, width)], second, pass_send, pass_recv, flip(bits[p][1]))
+
+    for g in range(PIECES):
+        for p in range(2):
+            far(p, g).start()
+    for g in range(PIECES):
+        for p in range(2):
+            mine(p, g).start()
+    for copy in loads:
+        copy.wait()
+    for g in range(PIECES):
+        for p in range(2):
+            span = pl.ds(g * width, width)
+            far(p, g).wait_recv()
+            passed[p, :, span] = near[p, :, span] + first_far[p, :, span]
+            onward(p, g).start()
+    for g in range(PIECES):
+        for p in range(2):
+            span = pl.ds(g * width, width)
+            mine(p, g).wait_recv()
+            rows = pl.ds(p * part, part)
+            own[rows, span] = own[rows, span] + first_own[p, :, span]
+    total = jnp.zeros((8, LANES), jnp.float32)
+    for g in range(PIECES):
+        for p in range(2):
+            span = pl.ds(g * width, width)
+            onward(p, g).wait_recv()
+            rows = pl.ds(p * part, part)
+            value = own[rows, span] + second[p, :, span]
+            own[rows, span] = value
+            square = value * value
+            for t in range(part // 8):
+                for c in range(width // LANES):
+                    total = total + square[8 * t:8 * t + 8, c * LANES:(c + 1) * LANES]
+    squares[pl.ds(me, 1), :] = jnp.sum(total, axis=0, keepdims=True)
+
+    def spread(step):
+        other = (me + step) % (nrows * nchan)
+        return pltpu.make_async_remote_copy(
+            src_ref=squares.at[pl.ds(me, 1)], dst_ref=squares.at[pl.ds(me, 1)], send_sem=square_send.at[step], recv_sem=square_recv.at[step],
+            device_id=(other % nchan, other // nchan), device_id_type=MESH)
+
+    def arrived(step):
+        other = (me + nrows * nchan - step) % (nrows * nchan)
+        return pltpu.make_async_remote_copy(
+            src_ref=squares.at[pl.ds(other, 1)], dst_ref=squares.at[pl.ds(other, 1)], send_sem=square_send.at[step], recv_sem=square_recv.at[step],
+            device_id=(other % nchan, other // nchan), device_id_type=MESH)
+
+    for step in range(1, nrows * nchan):
+        spread(step).start()
+    for step in range(1, nrows * nchan):
+        arrived(step).wait_recv()
+    everything = jnp.sum(jnp.sum(squares[...], axis=0, keepdims=True), axis=1, keepdims=True)
+    scale = lax.rsqrt(everything / count + 1e-06)
+    out[...] = own[...] * scale
+    for step in range(1, nrows * nchan):
+        spread(step).wait_send()
+    for g in range(PIECES):
+        for p in range(2):
+            far(p, g).wait_send()
+            mine(p, g).wait_send()
+            onward(p, g).wait_send()
+
+
+def sum_channels(nchan, nrows, image):
+    slab, ncols = image.shape[1:]
+    cols, part = ncols // nchan, slab // 2
+    dma, f32 = pltpu.SemaphoreType.DMA, jnp.float32
+    halves = pltpu.VMEM((2, part, cols), f32)
+    return pl.pallas_call(
+        functools.partial(sum_kernel, nchan, nrows, slab * nrows * ncols),
+        out_shape=jax.ShapeDtypeStruct((slab, cols), f32),
+        in_specs=[pl.BlockSpec(memory_space=pl.ANY)],
+        out_specs=pl.BlockSpec(memory_space=pltpu.VMEM),
+        scratch_shapes=[pltpu.VMEM((slab, cols), f32)] + [halves] * 5 + [pltpu.VMEM((nrows * nchan, LANES), f32), dma((3,))]
+        + [dma((2, PIECES))] * 6 + [dma((nrows * nchan,))] * 2,
+        compiler_params=pltpu.CompilerParams(collective_id=1, has_side_effects=True),
+        name="sum_channels",
+    )(image)
 
 
 def on_device(residual, psf, positions):
+    nchan, nrows = lax.axis_size("chan"), lax.axis_size("rows")
+    slab, ncols = residual.shape[1:]
+    shard, patch = psf.shape[1:]
+    central = nrows % 2 == 0 and slab * nrows == shard and 2 * shard * (nrows // 2) == patch
+    if not (central and nchan == 4 and slab % 16 == 0 and positions.shape[0] % 8 == 0 and positions.shape[0] <= LANES):
+        return on_any_device(residual, psf, positions)
+    start, couple = make_tables(positions, residual, psf)
+    win, amps = gather_patch(nchan, nrows, psf, start, couple)
+    image = apply_peaks(positions, amps, residual, win)
+    return (image, sum_channels(nchan, nrows, image))
+
+
+def on_any_device(residual, psf, positions):
     chan_id = lax.axis_index("chan")
     nchan = lax.axis_size("chan")
     row_id = lax.axis_index("rows")

time: 492 us -> 101 us (0.21)
  local copies, waits for them, and re-layouts: 139 us -> 3.23 us
  loops' own time: 108 us -> 0 us
  Pallas kernels: 0 us -> 97.1 us
  blocking collectives: 89.5 us -> 0 us
  other arithmetic: 68.9 us -> 0 us
  waiting for transfers between devices: 68.4 us -> 0 us
  between operations: 14.8 us -> 0.66 us
    another operation x2 -> x0, loops' own time: 108 us -> none  [the longest x1 85.1 us: on_device(): image = lax.fori_loop(0, STEPS, apply, image)]
    pallas_call x0 -> x4, Pallas kernels: none -> 97.1 us  [the longest x1 50.8 us: gather_patch(): pl.pallas_call(functools.partial(gather_kernel, nchan, nrows), out_shape=...]
    psum x2 -> x0, blocking collectives: 89.5 us -> none  [the longest x1 50 us: on_device(): lax.psum((chan_hot[:, None] * start_values[None, :], chan_hot[:, None, No...]
    dynamic_update_slice x64 -> x0, local copies, waits for them, and re-layouts: 67.2 us -> none  [the longest x32 64.1 us: subtract(): lax.dynamic_update_slice(image, window - scale * psf_rows, (zero, col - h...]
    dynamic_slice x64 -> x0, local copies, waits for them, and re-layouts: 39.7 us -> none  [apply(): return subtract(image, positions[k, 0], positions[k, 1], own_amps[k])]
    sub x33 -> x0, other arithmetic: 38.4 us -> none  [the longest x32 38.4 us: subtract(): window - scale * psf_rows]
    all_gather x1 -> x0, waiting for transfers between devices: 34.9 us -> none  [on_device(): full_psf = lax.all_gather(own_psf, 'rows', axis=0, tiled=True)]
    reduce_scatter x1 -> x0, waiting for transfers between devices: 33.5 us -> none  [on_device(): parts = lax.psum_scatter(image, 'chan', scatter_dimension=1, tiled=True)]
  transfers between devices with their start and end apart: 2 -> 0, of which waited for: 2 -> 0; matrix products, arithmetic and copies ran while one was open for 9% -> 0% of each run, Pallas kernels for 0% -> 0%
where the time goes in v1:
time: 101 us
  Pallas kernels  97.1 us (96%)
  local copies, waits for them, and re-layouts  3.23 us (3%)
    pallas_call x1, Pallas kernels, gather_patch(): pl.pallas_call(functools.partial(gather_kernel, nchan, nrows), out_shape=...  50.8 us
    pallas_call x1, Pallas kernels, sum_channels(): pl.pallas_call(functools.partial(sum_kernel, nchan, nrows, slab * nrows *...  29.1 us
    pallas_call x1, Pallas kernels, apply_peaks(): pl.pallas_call(apply_kernel, out_shape=jax.ShapeDtypeStruct(residual.shap...  13.9 us
    pallas_call x1, Pallas kernels, make_tables(): pl.pallas_call(table_kernel, out_shape=(jax.ShapeDtypeStruct((8, LANES),...  3.38 us
    unnamed x2, local copies, waits for them, and re-layouts  3.23 us

profile of v1, /device:TPU:0, one launch (start us, length us, event | category | flops | bytes accessed | tf_op | source)
XLA Modules:
  0.0 101.0 jit_solution(2217231819539124658)
XLA Ops:
  0.6 1.4 %copy.6.pos = s32[32,2]{1,0:T(8,128)} copy(s32[32,2]{0,1:T(2,128)} %param.5) | data formatting | bytes 512 | tf_op args[2]
  2.0 3.4 %make_tables.1 = (f32[8,128]{1,0:T(8,128)}, f32[32,128]{1,0:T(8,128)}) custom-call(s32[32,2]{1,0:T(8,128)} %copy.6.pos, f32[1,32,16384]{2,1,0:T(8,128)} %res.3, f32[1,256,2048]{2,1,0:T(8,128)} %psf.3), custom_call_target="tpu_custom_call" | custom-call | tf_op jit(solution)/shard_map/make_tables/pallas_call | solution.py:75
  5.4 50.8 %gather_patch.1 = (f32[320,2048]{1,0:T(8,128)}, f32[8,128]{1,0:T(8,128)}) custom-call(f32[1,256,2048]{2,1,0:T(8,128)} %psf.3, f32[8,128]{1,0:T(8,128)} %get-tuple-element.6.start_own, f32[32,128]{1,0:T(8,128)} %get-tuple-element.7.couple_own), custom_call_target="tpu_custom_call" | custom-call | tf_op jit(solution)/shard_map/gather_patch/pallas_call | solution.py:276
  56.2 13.9 %apply_peaks.1.image = f32[1,32,16384]{2,1,0:T(8,128)} custom-call(s32[32,2]{1,0:T(8,128)} %copy.6.pos, f32[8,128]{1,0:T(8,128)} %get-tuple-element.8.amps, f32[1,32,16384]{2,1,0:T(8,128)} %res.3, f32[320,2048]{1,0:T(8,128)} %get-tuple-element.9.win), custom_call_target="tpu_custom_call" | custom-call | tf_op jit(solution)/shard_map/apply_peaks/pallas_call | solution.py:336
  70.0 29.1 %sum_channels.1 = f32[32,4096]{1,0:T(8,128)} custom-call(f32[1,32,16384]{2,1,0:T(8,128)} %apply_peaks.1.image), custom_call_target="tpu_custom_call" | custom-call | tf_op jit(solution)/shard_map/sum_channels/pallas_call | solution.py:464
  99.1 1.9 %copy.8 = f32[32,4096]{1,0:T(8,128)} copy(f32[32,4096]{1,0:T(8,128)} %sum_channels.1) | data formatting | bytes 1048576

commit v2 on v1

--- a/solution.py
+++ b/solution.py
@@ -17,49 +17,68 @@
     return pl.ds(pl.multiple_of(start, 8), size)
 
 
-def pick(ref, row, col, wanted, lane_to, acc):
-    place = (pl.ds(pl.multiple_of((row >> 3) << 3, 8), 8), pl.ds(pl.multiple_of((col >> 7) << 7, LANES), LANES))
-    tile = pltpu.roll(ref[place], (lane_to - col) & (LANES - 1), 1)
-    number = lax.broadcasted_iota(jnp.int32, (8, LANES), 0) * LANES + lax.broadcasted_iota(jnp.int32, (8, LANES), 1)
-    return jnp.where(number == jnp.where(wanted, (row & 7) * LANES + lane_to, -1), tile, acc)
-
-
-def table_kernel(pos, res, psf, start, couple, res_v, psf_v, sems):
+def aligned(row, col):
+    return (pl.ds(pl.multiple_of((row >> 3) << 3, 8), 8), pl.ds(pl.multiple_of((col >> 7) << 7, LANES), LANES))
+
+
+def pick(tile, row, col, lane_to, number, acc):
+    moved = pltpu.roll(tile, (lane_to - col) & (LANES - 1), 1)
+    return jnp.where(number == (row & 7) * LANES + lane_to, moved, acc)
+
+
+def table_kernel(pos, res, psf, start, couple, tiles, psf_v, load_sem, sems):
     row, nrows = lax.axis_index("rows"), lax.axis_size("rows")
-    slab, steps = res.shape[1], pos.shape[0]
+    slab, steps = res.shape[1], pos.shape[1]
     shard, patch = psf.shape[1:]
     half = patch // 2
     first = row * slab
     is_root = jnp.logical_or(row == nrows // 2 - 1, row == nrows // 2)
-    loads = [pltpu.make_async_copy(res.at[0], res_v, sems.at[0]), pltpu.make_async_copy(psf.at[0], psf_v, sems.at[1])]
-    loads[0].start()
+    load = pltpu.make_async_copy(psf.at[0], psf_v, load_sem)
 
     @pl.when(is_root)
     def _():
-        loads[1].start()
-
-    loads[0].wait()
+        load.start()
+
+    loads = []
+    for k in range(steps):
+        rows, cols = aligned(jnp.clip(pos[0, k] - first, 0, slab - 1), pos[1, k])
+        loads.append(pltpu.make_async_copy(res.at[0, rows, cols], tiles.at[k], sems.at[k]))
+    for copy in loads:
+        copy.start()
+    lane = lax.broadcasted_iota(jnp.int32, (1, LANES), 1)
+    number = lax.broadcasted_iota(jnp.int32, (8, LANES), 0) * LANES + lax.broadcasted_iota(jnp.int32, (8, LANES), 1)
+    peak_rows, peak_cols = jnp.zeros((1, LANES), jnp.int32), jnp.zeros((1, LANES), jnp.int32)
+    for k in range(steps):
+        peak_rows = jnp.where(lane == k, pos[0, k], peak_rows)
+        peak_cols = jnp.where(lane == k, pos[1, k], peak_cols)
+    for copy in loads:
+        copy.wait()
     acc = jnp.zeros((8, LANES), jnp.float32)
     for k in range(steps):
-        r = pos[k, 0] - first
-        inside = jnp.logical_and(r >= 0, r < slab)
-        acc = pick(res_v, jnp.clip(r, 0, slab - 1), pos[k, 1], inside, k, acc)
-    start[...] = acc
+        acc = pick(tiles[k], pos[0, k] - first, pos[1, k], k, number, acc)
+    inside = (peak_rows >= first) & (peak_rows < first + slab) & (lane < steps)
+    start[...] = jnp.where(inside, acc, 0.0)
 
     @pl.when(is_root)
     def _():
-        loads[1].wait()
+        load.wait()
 
         def fill(k, carry):
-            line = jnp.zeros((8, LANES), jnp.float32)
-            rk = pos[k, 0] + half - row * shard
-            qk = pos[k, 1] + half
-            for j in range(steps):
-                r = rk - pos[j, 0]
-                c = qk - pos[j, 1]
-                owned = (r >= 0) & (r < shard) & (c >= 0) & (c < patch)
-                line = pick(psf_v, jnp.clip(r, 0, shard - 1), jnp.clip(c, 0, patch - 1), owned, j, line)
-            couple[pl.ds(k, 1), :] = jnp.sum(line, axis=0, keepdims=True)
+            rk = pos[0, k] + half - row * shard
+            qk = pos[1, k] + half
+
+            def group(g, line):
+                for i in range(8):
+                    j = g * 8 + i
+                    r = (rk - pos[0, j]) & (shard - 1)
+                    c = (qk - pos[1, j]) & (patch - 1)
+                    line = pick(psf_v[aligned(r, c)], r, c, j, number, line)
+                return line
+
+            line = lax.fori_loop(0, (k + 7) >> 3, group, jnp.zeros((8, LANES), jnp.float32))
+            r, c = rk - peak_rows, qk - peak_cols
+            owned = (r >= 0) & (r < shard) & (c >= 0) & (c < patch) & (lane < k)
+            couple[pl.ds(k, 1), :] = jnp.where(owned, jnp.sum(line, axis=0, keepdims=True), 0.0)
             return carry
 
         lax.fori_loop(0, steps, fill, 0)
@@ -74,10 +93,13 @@
     anywhere, vmem = pl.BlockSpec(memory_space=pl.ANY), pl.BlockSpec(memory_space=pltpu.VMEM)
     return pl.pallas_call(
         table_kernel,
-        out_shape=(jax.ShapeDtypeStruct((8, LANES), f32), jax.ShapeDtypeStruct((positions.shape[0], LANES), f32)),
+        out_shape=(jax.ShapeDtypeStruct((8, LANES), f32), jax.ShapeDtypeStruct((positions.shape[1], LANES), f32)),
         in_specs=[pl.BlockSpec(memory_space=pltpu.SMEM), anywhere, anywhere],
         out_specs=(vmem, vmem),
-        scratch_shapes=[pltpu.VMEM(residual.shape[1:], f32), pltpu.VMEM(psf.shape[1:], f32), pltpu.SemaphoreType.DMA((2,))],
+        scratch_shapes=[
+            pltpu.VMEM((positions.shape[1], 8, LANES), f32), pltpu.VMEM(psf.shape[1:], f32),
+            pltpu.SemaphoreType.DMA, pltpu.SemaphoreType.DMA((positions.shape[1],)),
+        ],
         name="make_tables",
     )(positions, residual, psf)
 
@@ -295,37 +317,51 @@
     slab, ncols = res.shape[1], res.shape[2]
     rows, patch = win.shape
     chunks = patch // LANES
+    tiles = slab // 8
     loads = [pltpu.make_async_copy(win.at[:, pl.ds(c * LANES, LANES)], patch_v.at[c], sems.at[c]) for c in range(chunks)]
-    loads.append(pltpu.make_async_copy(res.at[0], image.at[:, pl.ds(0, ncols)], sems.at[chunks]))
+
+    def band(t):
+        return pltpu.make_async_copy(res.at[0, pl.ds(8 * t, 8)], image.at[pl.ds(8 * t, 8), pl.ds(0, ncols)], sems.at[chunks + t])
+
+    def done(t):
+        return pltpu.make_async_copy(image.at[pl.ds(8 * t, 8), pl.ds(0, ncols)], out.at[0, pl.ds(8 * t, 8)], sems.at[chunks + tiles + t])
+
+    band(0).start()
     for copy in loads:
         copy.start()
+    for t in range(1, tiles):
+        band(t).start()
     for copy in loads:
         copy.wait()
     lane = lax.broadcasted_iota(jnp.int32, (8, LANES), 1)
     top = (row % 2) * slab + slab * nrows
 
-    def step(k, carry):
-        amp = amps[chan, k]
-        begin = top - pos[k, 0]
-        left = pos[k, 1] - patch // 2
-        shift = left & (LANES - 1)
-        base = left - shift
-        keep = lane < shift
-        for t in range(slab // 8):
-            before = jnp.zeros((8, LANES), jnp.float32)
-            for c in range(chunks + 1):
-                now = jnp.zeros((8, LANES), jnp.float32)
-                if c < chunks:
-                    now = pltpu.roll(patch_v[c, pl.ds(begin + 8 * t, 8), :] * amp, shift, 1)
-                place = (pl.ds(8 * t, 8), pl.ds(pl.multiple_of(base + c * LANES, LANES), LANES))
-                image[place] = image[place] - jnp.where(keep, before, now)
-                before = now
-        return carry
-
-    lax.fori_loop(0, pos.shape[0], step, 0)
-    store = pltpu.make_async_copy(image.at[:, pl.ds(0, ncols)], out.at[0], sems.at[0])
-    store.start()
-    store.wait()
+    for t in range(tiles):
+        band(t).wait()
+
+        def step(k, carry, t=t):
+            amp = amps[chan, k]
+            begin = top - pos[0, k] + 8 * t
+            left = pos[1, k] - patch // 2
+            shift = left & (LANES - 1)
+            base = left - shift
+            keep = lane < shift
+            moved = [pltpu.roll(patch_v[c, pl.ds(begin, 8), :] * amp, shift, 1) for c in range(chunks)]
+            places = [(pl.ds(8 * t, 8), pl.ds(pl.multiple_of(base + c * LANES, LANES), LANES)) for c in range(chunks + 1)]
+            values = [image[place] for place in places]
+            zero = jnp.zeros((8, LANES), jnp.float32)
+            for c, place in enumerate(places):
+                before = moved[c - 1] if c else zero
+                now = moved[c] if c < chunks else zero
+                values[c] = values[c] - jnp.where(keep, before, now)
+            for c, place in enumerate(places):
+                image[place] = values[c]
+            return carry
+
+        lax.fori_loop(0, pos.shape[1], step, 0)
+        done(t).start()
+    for t in range(tiles):
+        done(t).wait()
 
 
 def apply_peaks(positions, amps, residual, win):
@@ -340,13 +376,13 @@
         out_specs=anywhere,
         scratch_shapes=[
             pltpu.VMEM((slab, ncols + LANES), jnp.float32), pltpu.VMEM((chunks, rows, LANES), jnp.float32),
-            pltpu.SemaphoreType.DMA((chunks + 1,)),
+            pltpu.SemaphoreType.DMA((chunks + slab // 4,)),
         ],
         name="apply_peaks",
     )(positions, amps, residual, win)
 
 
-def sum_kernel(nchan, nrows, count, image, out, own, near, first_far, first_own, passed, second, squares,
+def sum_kernel(nchan, nrows, image, out, total_out, own, near, first_far, first_own, passed, second, squares,
                load_sem, far_send, far_recv, own_send, own_recv, pass_send, pass_recv, square_send, square_recv):
     chan, row = lax.axis_index("chan"), lax.axis_index("rows")
     me = row * nchan + chan
@@ -442,11 +478,13 @@
 
     for step in range(1, nrows * nchan):
         spread(step).start()
+    keep = pltpu.make_async_copy(own, out, load_sem.at[0])
+    keep.start()
     for step in range(1, nrows * nchan):
         arrived(step).wait_recv()
     everything = jnp.sum(jnp.sum(squares[...], axis=0, keepdims=True), axis=1, keepdims=True)
-    scale = lax.rsqrt(everything / count + 1e-06)
-    out[...] = own[...] * scale
+    total_out[...] = jnp.broadcast_to(everything, total_out.shape)
+    keep.wait()
     for step in range(1, nrows * nchan):
         spread(step).wait_send()
     for g in range(PIECES):
@@ -461,16 +499,17 @@
     cols, part = ncols // nchan, slab // 2
     dma, f32 = pltpu.SemaphoreType.DMA, jnp.float32
     halves = pltpu.VMEM((2, part, cols), f32)
-    return pl.pallas_call(
-        functools.partial(sum_kernel, nchan, nrows, slab * nrows * ncols),
-        out_shape=jax.ShapeDtypeStruct((slab, cols), f32),
+    parts, total = pl.pallas_call(
+        functools.partial(sum_kernel, nchan, nrows),
+        out_shape=(jax.ShapeDtypeStruct((slab, cols), f32), jax.ShapeDtypeStruct((8, LANES), f32)),
         in_specs=[pl.BlockSpec(memory_space=pl.ANY)],
-        out_specs=pl.BlockSpec(memory_space=pltpu.VMEM),
+        out_specs=(pl.BlockSpec(memory_space=pl.ANY), pl.BlockSpec(memory_space=pltpu.VMEM)),
         scratch_shapes=[pltpu.VMEM((slab, cols), f32)] + [halves] * 5 + [pltpu.VMEM((nrows * nchan, LANES), f32), dma((3,))]
         + [dma((2, PIECES))] * 6 + [dma((nrows * nchan,))] * 2,
         compiler_params=pltpu.CompilerParams(collective_id=1, has_side_effects=True),
         name="sum_channels",
     )(image)
+    return parts * lax.rsqrt(total[0, 0] / (slab * nrows * ncols) + 1e-06)
 
 
 def on_device(residual, psf, positions):
@@ -478,8 +517,10 @@
     slab, ncols = residual.shape[1:]
     shard, patch = psf.shape[1:]
     central = nrows % 2 == 0 and slab * nrows == shard and 2 * shard * (nrows // 2) == patch
-    if not (central and nchan == 4 and slab % 16 == 0 and positions.shape[0] % 8 == 0 and positions.shape[0] <= LANES):
+    powers = shard & (shard - 1) == 0 and patch & (patch - 1) == 0
+    if not (central and powers and nchan == 4 and slab % 16 == 0 and positions.shape[0] % 8 == 0 and positions.shape[0] <= LANES):
         return on_any_device(residual, psf, positions)
+    positions = positions.T
     start, couple = make_tables(positions, residual, psf)
     win, amps = gather_patch(nchan, nrows, psf, start, couple)
     image = apply_peaks(positions, amps, residual, win)

time: 101 us -> 98.1 us (0.971)
  Pallas kernels: 97.1 us -> 93.2 us
  local copies, waits for them, and re-layouts: 3.23 us -> 1.19 us
  other arithmetic: 0 us -> 1.87 us
    pallas_call x1, Pallas kernels: 50.8 us -> 46.9 us  [gather_patch(): pl.pallas_call(functools.partial(gather_kernel, nchan, nrows), out_shape=...]
    unnamed x2 -> x0, local copies, waits for them, and re-layouts: 3.23 us -> none
    mul x0 -> x1, other arithmetic: none -> 1.87 us  [sum_channels(): return parts * lax.rsqrt(total[0, 0] / (slab * nrows * ncols) + 1e-06)]
    slice x0 -> x1, local copies, waits for them, and re-layouts: none -> 1.19 us  [sum_channels(): return parts * lax.rsqrt(total[0, 0] / (slab * nrows * ncols) + 1e-06)]
where the time goes in v2:
time: 98.1 us; the launch traced here: 97.6 us
  Pallas kernels  93.2 us (95%)
  other arithmetic  1.87 us (2%)
  between operations  1.35 us (1%)
  local copies, waits for them, and re-layouts  1.19 us (1%)
    pallas_call x1, Pallas kernels, gather_patch(): pl.pallas_call(functools.partial(gather_kernel, nchan, nrows), out_shape=...  46.9 us
    pallas_call x1, Pallas kernels, sum_channels(): pl.pallas_call(functools.partial(sum_kernel, nchan, nrows), out_shape=(ja...  28.8 us
    pallas_call x1, Pallas kernels, apply_peaks(): pl.pallas_call(apply_kernel, out_shape=jax.ShapeDtypeStruct(residual.shap...  14.8 us
    pallas_call x1, Pallas kernels, make_tables(): pl.pallas_call(table_kernel, out_shape=(jax.ShapeDtypeStruct((8, LANES),...  2.66 us

profile of v2, /device:TPU:0, one launch (start us, length us, event | category | flops | bytes accessed | tf_op | source)
XLA Modules:
  0.0 97.6 jit_solution(10079588354114991786)
XLA Ops:
  0.6 2.7 %make_tables.1 = (f32[8,128]{1,0:T(8,128)}, f32[32,128]{1,0:T(8,128)}) custom-call(s32[2,32]{1,0:T(2,128)} %bitcast.2, f32[1,32,16384]{2,1,0:T(8,128)} %res.3, f32[1,256,2048]{2,1,0:T(8,128)} %psf.3), custom_call_target="tpu_custom_call" | custom-call | tf_op jit(solution)/shard_map/make_tables/pallas_call | solution.py:94
  3.3 46.9 %gather_patch.1 = (f32[320,2048]{1,0:T(8,128)}, f32[8,128]{1,0:T(8,128)}) custom-call(f32[1,256,2048]{2,1,0:T(8,128)} %psf.3, f32[8,128]{1,0:T(8,128)} %get-tuple-element.8.start_own, f32[32,128]{1,0:T(8,128)} %get-tuple-element.9.couple_own), custom_call_target="tpu_custom_call" | custom-call | tf_op jit(solution)/shard_map/gather_patch/pallas_call | solution.py:298
  50.2 14.8 %apply_peaks.1.image = f32[1,32,16384]{2,1,0:T(8,128)} custom-call(s32[2,32]{1,0:T(2,128)} %bitcast.3, f32[8,128]{1,0:T(8,128)} %get-tuple-element.10.amps, f32[1,32,16384]{2,1,0:T(8,128)} %res.3, f32[320,2048]{1,0:T(8,128)} %get-tuple-element.11.win), custom_call_target="tpu_custom_call" | custom-call | tf_op jit(solution)/shard_map/apply_peaks/pallas_call | solution.py:372
  65.0 28.8 %sum_channels.1 = (f32[32,4096]{1,0:T(8,128)}, f32[8,128]{1,0:T(8,128)}) custom-call(f32[1,32,16384]{2,1,0:T(8,128)} %apply_peaks.1.image), custom_call_target="tpu_custom_call" | custom-call | tf_op jit(solution)/shard_map/sum_channels/pallas_call | solution.py:502
  93.9 1.2 %slice.3 = f32[1,1]{1,0:T(1,128)} slice(f32[8,128]{1,0:T(8,128)} %get-tuple-element.13), slice={[0:1], [0:1]} | slice | bytes 8 | tf_op jit(solution)/shard_map/slice | solution.py:512
  95.7 1.9 %broadcast_multiply_fusion = f32[32,4096]{1,0:T(8,128)} fusion(f32[32,4096]{1,0:T(8,128)} %get-tuple-element.12, f32[]{:T(128)} %bitcast.1), kind=kLoop, calls=%fused_computation | loop fusion | flops 131072 | bytes 1048580 | tf_op jit(solution)/shard_map/mul | solution.py:512

commit v3 on v2

--- a/solution.py
+++ b/solution.py
@@ -26,7 +26,7 @@
     return jnp.where(number == (row & 7) * LANES + lane_to, moved, acc)
 
 
-def table_kernel(pos, res, psf, start, couple, tiles, psf_v, load_sem, sems):
+def table_kernel(pos, res, psf, start, couple, tiles, psf_v, grid, pairs, load_sem, sems):
     row, nrows = lax.axis_index("rows"), lax.axis_size("rows")
     slab, steps = res.shape[1], pos.shape[1]
     shard, patch = psf.shape[1:]
@@ -61,27 +61,31 @@
 
     @pl.when(is_root)
     def _():
+        grid[...] = jnp.zeros_like(grid)
+        low = row * shard - half
+
+        def listed(k, found):
+            rk, qk = pos[0, k] - low, pos[1, k] + half
+
+            def test(j, found):
+                r, c = rk - pos[0, j], qk - pos[1, j]
+                owned = (r >= 0) & (r < shard) & (c >= 0) & (c < patch)
+                pairs[found] = k * steps + j
+                return found + owned.astype(jnp.int32)
+
+            return lax.fori_loop(0, k, test, found)
+
+        found = lax.fori_loop(0, steps, listed, jnp.int32(0))
         load.wait()
 
-        def fill(k, carry):
-            rk = pos[0, k] + half - row * shard
-            qk = pos[1, k] + half
-
-            def group(g, line):
-                for i in range(8):
-                    j = g * 8 + i
-                    r = (rk - pos[0, j]) & (shard - 1)
-                    c = (qk - pos[1, j]) & (patch - 1)
-                    line = pick(psf_v[aligned(r, c)], r, c, j, number, line)
-                return line
-
-            line = lax.fori_loop(0, (k + 7) >> 3, group, jnp.zeros((8, LANES), jnp.float32))
-            r, c = rk - peak_rows, qk - peak_cols
-            owned = (r >= 0) & (r < shard) & (c >= 0) & (c < patch) & (lane < k)
-            couple[pl.ds(k, 1), :] = jnp.where(owned, jnp.sum(line, axis=0, keepdims=True), 0.0)
+        def fill(n, carry):
+            k, j = pairs[n] // steps, pairs[n] % steps
+            r, c = pos[0, k] - low - pos[0, j], pos[1, k] + half - pos[1, j]
+            grid[k] = pick(psf_v[aligned(r, c)], r, c, j, number, grid[k])
             return carry
 
-        lax.fori_loop(0, steps, fill, 0)
+        lax.fori_loop(0, found, fill, 0)
+        couple[...] = jnp.sum(grid[...], axis=1)
 
     @pl.when(jnp.logical_not(is_root))
     def _():
@@ -98,6 +102,7 @@
         out_specs=(vmem, vmem),
         scratch_shapes=[
             pltpu.VMEM((positions.shape[1], 8, LANES), f32), pltpu.VMEM(psf.shape[1:], f32),
+            pltpu.VMEM((positions.shape[1], 8, LANES), f32), pltpu.SMEM((positions.shape[1] ** 2,), jnp.int32),
             pltpu.SemaphoreType.DMA, pltpu.SemaphoreType.DMA((positions.shape[1],)),
         ],
         name="make_tables",
@@ -336,30 +341,28 @@
     lane = lax.broadcasted_iota(jnp.int32, (8, LANES), 1)
     top = (row % 2) * slab + slab * nrows
 
-    for t in range(tiles):
-        band(t).wait()
-
-        def step(k, carry, t=t):
+    zero = jnp.zeros((8, LANES), jnp.float32)
+    for pair in range(tiles // 2):
+        mine = (2 * pair, 2 * pair + 1)
+        for t in mine:
+            band(t).wait()
+
+        def step(k, carry, mine=mine):
             amp = amps[chan, k]
-            begin = top - pos[0, k] + 8 * t
+            begin = top - pos[0, k]
             left = pos[1, k] - patch // 2
             shift = left & (LANES - 1)
-            base = left - shift
+            span = pl.ds(pl.multiple_of(left - shift, LANES), patch + LANES)
             keep = lane < shift
-            moved = [pltpu.roll(patch_v[c, pl.ds(begin, 8), :] * amp, shift, 1) for c in range(chunks)]
-            places = [(pl.ds(8 * t, 8), pl.ds(pl.multiple_of(base + c * LANES, LANES), LANES)) for c in range(chunks + 1)]
-            values = [image[place] for place in places]
-            zero = jnp.zeros((8, LANES), jnp.float32)
-            for c, place in enumerate(places):
-                before = moved[c - 1] if c else zero
-                now = moved[c] if c < chunks else zero
-                values[c] = values[c] - jnp.where(keep, before, now)
-            for c, place in enumerate(places):
-                image[place] = values[c]
+            for t in mine:
+                moved = [zero] + [pltpu.roll(patch_v[c, pl.ds(begin + 8 * t, 8), :] * amp, shift, 1) for c in range(chunks)] + [zero]
+                change = jnp.concatenate([jnp.where(keep, moved[c], moved[c + 1]) for c in range(chunks + 1)], axis=1)
+                image[pl.ds(8 * t, 8), span] = image[pl.ds(8 * t, 8), span] - change
             return carry
 
         lax.fori_loop(0, pos.shape[1], step, 0)
-        done(t).start()
+        for t in mine:
+            done(t).start()
     for t in range(tiles):
         done(t).wait()
 

time: 98.1 us -> 94.4 us (0.962)
  Pallas kernels: 93.2 us -> 89.1 us
    pallas_call x1, Pallas kernels: 14.8 us -> 10.7 us  [apply_peaks(): pl.pallas_call(apply_kernel, out_shape=jax.ShapeDtypeStruct(residual.shap...]
where the time goes in v3:
time: 94.4 us; the launch traced here: 93.5 us
  Pallas kernels  89.1 us (94%)
  other arithmetic  1.87 us (2%)
  between operations  1.35 us (1%)
  local copies, waits for them, and re-layouts  1.19 us (1%)
    pallas_call x1, Pallas kernels, gather_patch(): pl.pallas_call(functools.partial(gather_kernel, nchan, nrows), out_shape=...  47.4 us
    pallas_call x1, Pallas kernels, sum_channels(): pl.pallas_call(functools.partial(sum_kernel, nchan, nrows), out_shape=(ja...  28.4 us
    pallas_call x1, Pallas kernels, apply_peaks(): pl.pallas_call(apply_kernel, out_shape=jax.ShapeDtypeStruct(residual.shap...  10.7 us
    pallas_call x1, Pallas kernels, make_tables(): pl.pallas_call(table_kernel, out_shape=(jax.ShapeDtypeStruct((8, LANES),...  2.66 us

profile of v3, /device:TPU:0, one launch (start us, length us, event | category | flops | bytes accessed | tf_op | source)
XLA Modules:
  0.0 93.5 jit_solution(8404102983299168837)
XLA Ops:
  0.6 2.7 %make_tables.1 = (f32[8,128]{1,0:T(8,128)}, f32[32,128]{1,0:T(8,128)}) custom-call(s32[2,32]{1,0:T(2,128)} %bitcast.2, f32[1,32,16384]{2,1,0:T(8,128)} %res.3, f32[1,256,2048]{2,1,0:T(8,128)} %psf.3), custom_call_target="tpu_custom_call" | custom-call | tf_op jit(solution)/shard_map/make_tables/pallas_call | solution.py:98
  3.3 47.4 %gather_patch.1 = (f32[320,2048]{1,0:T(8,128)}, f32[8,128]{1,0:T(8,128)}) custom-call(f32[1,256,2048]{2,1,0:T(8,128)} %psf.3, f32[8,128]{1,0:T(8,128)} %get-tuple-element.8.start_own, f32[32,128]{1,0:T(8,128)} %get-tuple-element.9.couple_own), custom_call_target="tpu_custom_call" | custom-call | tf_op jit(solution)/shard_map/gather_patch/pallas_call | solution.py:303
  50.7 10.7 %apply_peaks.1.image = f32[1,32,16384]{2,1,0:T(8,128)} custom-call(s32[2,32]{1,0:T(2,128)} %bitcast.3, f32[8,128]{1,0:T(8,128)} %get-tuple-element.10.amps, f32[1,32,16384]{2,1,0:T(8,128)} %res.3, f32[320,2048]{1,0:T(8,128)} %get-tuple-element.11.win), custom_call_target="tpu_custom_call" | custom-call | tf_op jit(solution)/shard_map/apply_peaks/pallas_call | solution.py:375
  61.4 28.4 %sum_channels.1 = (f32[32,4096]{1,0:T(8,128)}, f32[8,128]{1,0:T(8,128)}) custom-call(f32[1,32,16384]{2,1,0:T(8,128)} %apply_peaks.1.image), custom_call_target="tpu_custom_call" | custom-call | tf_op jit(solution)/shard_map/sum_channels/pallas_call | solution.py:505
  89.8 1.2 %slice.3 = f32[1,1]{1,0:T(1,128)} slice(f32[8,128]{1,0:T(8,128)} %get-tuple-element.13), slice={[0:1], [0:1]} | slice | bytes 8 | tf_op jit(solution)/shard_map/slice | solution.py:515
  91.7 1.9 %broadcast_multiply_fusion = f32[32,4096]{1,0:T(8,128)} fusion(f32[32,4096]{1,0:T(8,128)} %get-tuple-element.12, f32[]{:T(128)} %bitcast.1), kind=kLoop, calls=%fused_computation | loop fusion | flops 131072 | bytes 1048580 | tf_op jit(solution)/shard_map/mul | solution.py:515

commit v4 on v3

--- a/solution.py
+++ b/solution.py
@@ -67,13 +67,16 @@
         def listed(k, found):
             rk, qk = pos[0, k] - low, pos[1, k] + half
 
-            def test(j, found):
-                r, c = rk - pos[0, j], qk - pos[1, j]
-                owned = (r >= 0) & (r < shard) & (c >= 0) & (c < patch)
-                pairs[found] = k * steps + j
-                return found + owned.astype(jnp.int32)
-
-            return lax.fori_loop(0, k, test, found)
+            def test(g, found):
+                for i in range(8):
+                    j = g * 8 + i
+                    r, c = rk - pos[0, j], qk - pos[1, j]
+                    owned = (r >= 0) & (r < shard) & (c >= 0) & (c < patch) & (j < k)
+                    pairs[found] = k * steps + j
+                    found = found + owned.astype(jnp.int32)
+                return found
+
+            return lax.fori_loop(0, (k + 7) >> 3, test, found)
 
         found = lax.fori_loop(0, steps, listed, jnp.int32(0))
         load.wait()

time: 94.4 us -> 93.4 us (0.989)
    pallas_call x1, Pallas kernels: 47.4 us -> 46.4 us  [gather_patch(): pl.pallas_call(functools.partial(gather_kernel, nchan, nrows), out_shape=...]
where the time goes in v4:
time: 93.4 us; the launch traced here: 93.3 us
  Pallas kernels  88.9 us (95%)
  other arithmetic  1.87 us (2%)
  between operations  1.35 us (1%)
  local copies, waits for them, and re-layouts  1.19 us (1%)
    pallas_call x1, Pallas kernels, gather_patch(): pl.pallas_call(functools.partial(gather_kernel, nchan, nrows), out_shape=...  46.4 us
    pallas_call x1, Pallas kernels, sum_channels(): pl.pallas_call(functools.partial(sum_kernel, nchan, nrows), out_shape=(ja...  29.1 us
    pallas_call x1, Pallas kernels, apply_peaks(): pl.pallas_call(apply_kernel, out_shape=jax.ShapeDtypeStruct(residual.shap...  10.7 us
    pallas_call x1, Pallas kernels, make_tables(): pl.pallas_call(table_kernel, out_shape=(jax.ShapeDtypeStruct((8, LANES),...  2.66 us
    mul x1, other arithmetic, sum_channels(): return parts * lax.rsqrt(total[0, 0] / (slab * nrows * ncols) + 1e-06)  1.87 us

profile of v4, /device:TPU:0, one launch (start us, length us, event | category | flops | bytes accessed | tf_op | source)
XLA Modules:
  0.0 93.3 jit_solution(15623742310056886061)
XLA Ops:
  0.6 2.7 %make_tables.1 = (f32[8,128]{1,0:T(8,128)}, f32[32,128]{1,0:T(8,128)}) custom-call(s32[2,32]{1,0:T(2,128)} %bitcast.2, f32[1,32,16384]{2,1,0:T(8,128)} %res.3, f32[1,256,2048]{2,1,0:T(8,128)} %psf.3), custom_call_target="tpu_custom_call" | custom-call | tf_op jit(solution)/shard_map/make_tables/pallas_call | solution.py:101
  3.3 46.4 %gather_patch.1 = (f32[320,2048]{1,0:T(8,128)}, f32[8,128]{1,0:T(8,128)}) custom-call(f32[1,256,2048]{2,1,0:T(8,128)} %psf.3, f32[8,128]{1,0:T(8,128)} %get-tuple-element.8.start_own, f32[32,128]{1,0:T(8,128)} %get-tuple-element.9.couple_own), custom_call_target="tpu_custom_call" | custom-call | tf_op jit(solution)/shard_map/gather_patch/pallas_call | solution.py:306
  49.7 10.7 %apply_peaks.1.image = f32[1,32,16384]{2,1,0:T(8,128)} custom-call(s32[2,32]{1,0:T(2,128)} %bitcast.3, f32[8,128]{1,0:T(8,128)} %get-tuple-element.10.amps, f32[1,32,16384]{2,1,0:T(8,128)} %res.3, f32[320,2048]{1,0:T(8,128)} %get-tuple-element.11.win), custom_call_target="tpu_custom_call" | custom-call | tf_op jit(solution)/shard_map/apply_peaks/pallas_call | solution.py:378
  60.4 29.1 %sum_channels.1 = (f32[32,4096]{1,0:T(8,128)}, f32[8,128]{1,0:T(8,128)}) custom-call(f32[1,32,16384]{2,1,0:T(8,128)} %apply_peaks.1.image), custom_call_target="tpu_custom_call" | custom-call | tf_op jit(solution)/shard_map/sum_channels/pallas_call | solution.py:508
  89.6 1.2 %slice.3 = f32[1,1]{1,0:T(1,128)} slice(f32[8,128]{1,0:T(8,128)} %get-tuple-element.13), slice={[0:1], [0:1]} | slice | bytes 8 | tf_op jit(solution)/shard_map/slice | solution.py:518
  91.4 1.9 %broadcast_multiply_fusion = f32[32,4096]{1,0:T(8,128)} fusion(f32[32,4096]{1,0:T(8,128)} %get-tuple-element.12, f32[]{:T(128)} %bitcast.1), kind=kLoop, calls=%fused_computation | loop fusion | flops 131072 | bytes 1048580 | tf_op jit(solution)/shard_map/mul | solution.py:518
